TPU v7x, 32 devices: a 4x2x2 block of a 4x4x8 slice. The times are simulated.
32 devices in a mesh: dp: 4 (over y, z), tp: 8 (over x, core).
Axes of the slice: x: 4, y: 2, z: 2, core: 2. Of those that a mesh axis runs over, the one named last changes fastest.
The devices are a block of a 4x4x8 slice.
Arguments:
- hidden_in: bfloat16 [4, 4096, 1024], P('dp', 'tp'), parts along dimension 0
- norms: float32 [2, 4, 1024], replicated
- w_qkv: bfloat16 [2, 1024, 3, 16, 64], P(None, None, None, 'tp')
- w_out: bfloat16 [2, 16, 64, 1024], P(None, 'tp')
- b_out: float32 [2, 1024], replicated
- w_up: bfloat16 [2, 1024, 4096], P(None, None, 'tp')
- b_up: float32 [2, 4096], P(None, 'tp')
- w_down: bfloat16 [2, 4096, 1024], P(None, 'tp')
- b_down: float32 [2, 1024], replicated
Outputs:
- output: bfloat16 [4, 4096, 1024], P('dp', 'tp'), parts along dimension 0
There are 4 independent parts. A program takes and returns all parts, laid end to end along the dimension named above; an argument that names none is the same for every part.
All inputs are finite; a program needn't handle non-finite values.
Results may differ from a plain program's by a relative error of at most 0.0109788.
Values are sent between devices in bfloat16 or wider.
A program may use at most 768 MiB of HBM per device.

v0:
```python
import jax
import jax.numpy as jnp
from jax import lax
from jax.sharding import PartitionSpec as P

LN_EPS = 1e-5


def layer_norm(rows, gain, shift):
    row_mean = jnp.mean(rows, axis=-1, keepdims=True)
    centred = rows - row_mean
    row_var = jnp.mean(centred * centred, axis=-1, keepdims=True)
    return (centred * lax.rsqrt(row_var + LN_EPS) * gain + shift).astype(jnp.bfloat16)


def attention(qkv_rows, head_dim):
    scores = jnp.einsum('bqhe,bkhe->bhqk', qkv_rows[:, :, 0], qkv_rows[:, :, 1], preferred_element_type=jnp.float32) * head_dim ** -0.5
    attn_prob = jax.nn.softmax(scores, axis=-1).astype(jnp.bfloat16)
    return jnp.einsum('bhqk,bkhe->bqhe', attn_prob, qkv_rows[:, :, 2], preferred_element_type=jnp.float32).astype(jnp.bfloat16)


def reduce_rows(partial, group_size):
    batch_loc, seq_len, width = partial.shape
    received = lax.all_to_all(partial.astype(jnp.bfloat16), 'tp', 1, 0, tiled=True)
    received = received.reshape(group_size, batch_loc, seq_len // group_size, width)
    return jnp.sum(received.astype(jnp.float32), axis=0)


def solution(mesh):
    group_size = mesh.shape['tp']

    def local_layers(hidden_in, norms, w_qkv, w_out, b_out, w_up, b_up, w_down, b_down):
        head_dim = w_qkv.shape[-1]
        residual = hidden_in.astype(jnp.float32)
        for layer_idx in range(w_qkv.shape[0]):
            normed = layer_norm(residual, norms[layer_idx, 0], norms[layer_idx, 1])
            full_rows = lax.all_gather(normed, 'tp', axis=1, tiled=True)
            qkv_rows = jnp.einsum('bsd,dthe->bsthe', full_rows, w_qkv[layer_idx], preferred_element_type=jnp.float32).astype(jnp.bfloat16)
            attn_rows = attention(qkv_rows, head_dim)
            partial = jnp.einsum('bshe,hed->bsd', attn_rows, w_out[layer_idx], preferred_element_type=jnp.float32)
            residual = residual + reduce_rows(partial, group_size) + b_out[layer_idx]
            normed2 = layer_norm(residual, norms[layer_idx, 2], norms[layer_idx, 3])
            full_rows2 = lax.all_gather(normed2, 'tp', axis=1, tiled=True)
            hidden = jnp.einsum('bsd,df->bsf', full_rows2, w_up[layer_idx], preferred_element_type=jnp.float32) + b_up[layer_idx]
            gelu_out = jax.nn.gelu(hidden, approximate=True).astype(jnp.bfloat16)
            partial2 = jnp.einsum('bsf,fd->bsd', gelu_out, w_down[layer_idx], preferred_element_type=jnp.float32)
            residual = residual + reduce_rows(partial2, group_size) + b_down[layer_idx]
        return residual.astype(jnp.bfloat16)

    in_specs = (P('dp', 'tp', None), P(), P(None, None, None, 'tp', None), P(None, 'tp', None, None), P(), P(None, None, 'tp'), P(None, 'tp'), P(None, 'tp', None), P())
    return jax.shard_map(local_layers, mesh=mesh, in_specs=in_specs, out_specs=P('dp', 'tp', None), check_vma=False)
```

profile of v0, /device:TPU:81, one launch (start us, length us, event | category | flops | bytes accessed | tf_op | source)
XLA Modules:
  0.0 1402.5 jit_solution(12000591487782299306)
XLA Ops:
  15.1 50.0 %all-gather.5.cloned.1.call-done = bf16[1,4096,1024]{2,1,0:T(8,128)(2,1)} async-done(((bf16[1,512,1024]{2,1,0:T(8,128)(2,1)}), bf16[1,4096,1024]{2,1,0:T(8,128)(2,1)}) %all-gather.5.cloned.1.call-update) | async-done | bytes 8388624 | tf_op jit(solution)/shard_map/all_gather | solution.py:37
  71.5 54.1 %fusion.113 = (f32[2,4096]{1,0:T(2,128)S(1)}, f32[2,4096,4096]{1,2,0:T(8,128)}) fusion(bf16[1,4096,3,2,64]{1,4,3,2,0:T(8,128)(2,1)S(1)} %convert_bitcast_fusion.3), kind=kOutput, calls=%fused_computation.133 | convolution fusion | flops 4395634688 | bytes 136347648 | tf_op jit(solution)/shard_map/sub | solution.py:18
  125.5 42.9 %fusion.48 = bf16[4096,2,64]{0,2,1:T(8,128)(2,1)} fusion(f32[2,4096,4096]{1,2,0:T(8,128)} %get-tuple-element.26, f32[2,4096]{1,0:T(2,128)S(1)} %get-tuple-element.25, bf16[1,4096,3,2,64]{1,4,3,2,0:T(8,128)(2,1)S(1)} %convert_bitcast_fusion.3), kind=kOutput, calls=%fused_computation.50 | convolution fusion | flops 4362600448 | bytes 136347648 | tf_op jit(solution)/shard_map/bhqk,bkhe->bqhe/dot_general | solution.py:19
  172.0 57.0 %copy.31 = bf16[1,4096,1024]{2,0,1:T(2,128)(2,1)} copy(bf16[1,4096,1024]{2,1,0:T(8,128)(2,1)S(1)} %fusion.40) | data formatting | bytes 16777216 | tf_op jit(solution)/shard_map/convert_element_type | solution.py:24
  229.5 49.5 %reduce.24 = bf16[4096,1024]{1,0:T(8,128)(2,1)} reduce(bf16[4096,1,1024]{2,1,0:T(2,128)(2,1)} %bitcast.198, bf16[]{:T(256)} %broadcast.201), dimensions={1}, to_apply=%bitcast.197.reduce_sub_computation | reduce | bytes 16777218
  278.9 11.2 reshape.350
  296.0 93.0 %all-to-all-done = bf16[8,2,262144]{2,1,0:T(2,128)(2,1)} async-done(((bf16[8,2,262144]{2,1,0:T(2,128)(2,1)}), bf16[8,2,262144]{2,1,0:T(2,128)(2,1)}, u32[]{:S(2)}, u32[]{:S(2)}) %all-to-all-start) | async-done | bytes 8388640 | tf_op jit(solution)/shard_map/all_to_all | solution.py:24
  389.0 13.5 reshape.351
  402.4 14.1 %copy.20 = f32[1,4096,1024]{2,1,0:T(8,128)} copy(bf16[1,4096,1024]{2,0,1:T(2,128)(2,1)} %bitcast.201) | data formatting | bytes 25165824
  427.6 46.1 %all-gather.7.cloned.1.call-done = bf16[1,4096,1024]{2,1,0:T(8,128)(2,1)} async-done(((bf16[1,512,1024]{2,1,0:T(8,128)(2,1)}), bf16[1,4096,1024]{2,1,0:T(8,128)(2,1)}) %all-gather.7.cloned.1.call-update) | async-done | bytes 8388624 | tf_op jit(solution)/shard_map/all_gather | solution.py:43
  473.8 15.4 %convert_bitcast_fusion.1 = bf16[1,4096,1024]{2,1,0:T(8,128)(2,1)} fusion(bf16[1,4096,1024]{2,1,0:T(8,128)(2,1)} %all-gather.7.cloned.1.call-done, f32[512]{0:T(512)S(1)} %bitcast.230, bf16[2,512,1024]{2,1,0:T(8,128)(2,1)} %param.16, bf16[2,1024,512]{2,1,0:T(8,128)(2,1)} %param.14), kind=kOutput, calls=%fused_computation.45 | convolution fusion | flops 8615100416 | bytes 18876416 | tf_op jit(solution)/shard_map/bsf,fd->bsd/dot_general | solution.py:46
  489.2 15.8 %copy.30 = bf16[1,4096,1024]{2,0,1:T(2,128)(2,1)} copy(bf16[1,4096,1024]{2,1,0:T(8,128)(2,1)} %convert_bitcast_fusion.1) | data formatting | bytes 16777216 | tf_op jit(solution)/shard_map/convert_element_type | solution.py:24
  505.0 49.5 %reduce.25 = bf16[4096,1024]{1,0:T(8,128)(2,1)} reduce(bf16[4096,1,1024]{2,1,0:T(2,128)(2,1)} %bitcast.203, bf16[]{:T(256)} %broadcast.201), dimensions={1}, to_apply=%bitcast.196.reduce_sub_computation | reduce | bytes 16777218
  571.5 93.0 %all-to-all-done.1 = bf16[8,2,262144]{2,1,0:T(2,128)(2,1)} async-done(((bf16[8,2,262144]{2,1,0:T(2,128)(2,1)}), bf16[8,2,262144]{2,1,0:T(2,128)(2,1)}, u32[]{:S(2)}, u32[]{:S(2)}) %all-to-all-start.1) | async-done | bytes 8388640 | tf_op jit(solution)/shard_map/all_to_all | solution.py:24
  664.5 13.3 reshape.353
  677.8 14.1 %copy.21 = f32[1,4096,1024]{2,1,0:T(8,128)} copy(bf16[1,4096,1024]{2,0,1:T(2,128)(2,1)} %bitcast.204) | data formatting | bytes 25165824
  706.2 46.7 %all-gather.9.cloned.1.call-done = bf16[1,4096,1024]{2,1,0:T(8,128)(2,1)} async-done(((bf16[1,512,1024]{2,1,0:T(8,128)(2,1)}), bf16[1,4096,1024]{2,1,0:T(8,128)(2,1)}) %all-gather.9.cloned.1.call-update) | async-done | bytes 8388624 | tf_op jit(solution)/shard_map/all_gather | solution.py:37
  759.3 54.0 %fusion.114 = (f32[2,4096]{1,0:T(2,128)S(1)}, f32[2,4096,4096]{1,2,0:T(8,128)}) fusion(bf16[1,4096,3,2,64]{1,4,3,2,0:T(8,128)(2,1)S(1)} %convert_bitcast_fusion.2), kind=kOutput, calls=%fused_computation.134 | convolution fusion | flops 4395634688 | bytes 136347648 | tf_op jit(solution)/shard_map/sub | solution.py:18
  813.4 42.9 %fusion.49 = bf16[4096,2,64]{0,2,1:T(8,128)(2,1)} fusion(f32[2,4096,4096]{1,2,0:T(8,128)} %get-tuple-element.28, f32[2,4096]{1,0:T(2,128)S(1)} %get-tuple-element.27, bf16[1,4096,3,2,64]{1,4,3,2,0:T(8,128)(2,1)S(1)} %convert_bitcast_fusion.2), kind=kOutput, calls=%fused_computation.51 | convolution fusion | flops 4362600448 | bytes 136347648 | tf_op jit(solution)/shard_map/bhqk,bkhe->bqhe/dot_general | solution.py:19
  859.9 56.5 %copy.29 = bf16[1,4096,1024]{2,0,1:T(2,128)(2,1)} copy(bf16[1,4096,1024]{2,1,0:T(8,128)(2,1)S(1)} %fusion.41) | data formatting | bytes 16777216 | tf_op jit(solution)/shard_map/convert_element_type | solution.py:24
  916.4 49.5 %reduce.26 = bf16[4096,1024]{1,0:T(8,128)(2,1)} reduce(bf16[4096,1,1024]{2,1,0:T(2,128)(2,1)} %bitcast.206, bf16[]{:T(256)} %broadcast.201), dimensions={1}, to_apply=%bitcast.195.reduce_sub_computation | reduce | bytes 16777218
  965.8 11.2 reshape.354
  977.0 99.8 %all_to_all.16 = bf16[8,2,262144]{2,1,0:T(2,128)(2,1)} all-to-all(bf16[8,2,262144]{2,1,0:T(2,128)(2,1)} %reshape.354), channel_id=1, replica_groups=mesh['dp'=4,'tp'=8] {'tp'}, dimensions={0} | all-to-all | bytes 16777216 | tf_op jit(solution)/shard_map/all_to_all | solution.py:24
  1076.8 13.3 reshape.355
  1090.1 14.1 %copy.22 = f32[1,4096,1024]{2,1,0:T(8,128)} copy(bf16[1,4096,1024]{2,0,1:T(2,128)(2,1)} %bitcast.207) | data formatting | bytes 25165824
  1118.3 46.8 %all-gather.11.cloned.1.call-done = bf16[1,4096,1024]{2,1,0:T(8,128)(2,1)} async-done(((bf16[1,512,1024]{2,1,0:T(8,128)(2,1)}), bf16[1,4096,1024]{2,1,0:T(8,128)(2,1)}) %all-gather.11.cloned.1.call-update) | async-done | bytes 8388624 | tf_op jit(solution)/shard_map/all_gather | solution.py:43
  1165.1 15.1 %convert_bitcast_fusion = bf16[1,4096,1024]{2,1,0:T(8,128)(2,1)} fusion(bf16[1,4096,1024]{2,1,0:T(8,128)(2,1)} %all-gather.11.cloned.1.call-done, f32[512]{0:T(512)S(1)} %bitcast.229, bf16[2,512,1024]{2,1,0:T(8,128)(2,1)S(1)} %copy-done.19, bf16[2,1024,512]{2,1,0:T(8,128)(2,1)} %param.14), kind=kOutput, calls=%fused_computation.44 | convolution fusion | flops 8615100416 | bytes 18876416 | tf_op jit(solution)/shard_map/bsf,fd->bsd/dot_general | solution.py:46
  1180.2 15.6 %copy.28 = bf16[1,4096,1024]{2,0,1:T(2,128)(2,1)} copy(bf16[1,4096,1024]{2,1,0:T(8,128)(2,1)} %convert_bitcast_fusion) | data formatting | bytes 16777216 | tf_op jit(solution)/shard_map/convert_element_type | solution.py:24
  1195.9 49.5 %reduce.27 = bf16[4096,1024]{1,0:T(8,128)(2,1)} reduce(bf16[4096,1,1024]{2,1,0:T(2,128)(2,1)} %bitcast.199, bf16[]{:T(256)} %broadcast.201), dimensions={1}, to_apply=%bitcast.194.reduce_sub_computation | reduce | bytes 16777218
  1256.5 99.3 %all_to_all.17 = bf16[8,2,262144]{2,1,0:T(2,128)(2,1)} all-to-all(bf16[8,2,262144]{2,1,0:T(2,128)(2,1)} %reshape.356), channel_id=1, replica_groups=mesh['dp'=4,'tp'=8] {'tp'}, dimensions={0} | all-to-all | bytes 16777216 | tf_op jit(solution)/shard_map/all_to_all | solution.py:24
  1355.8 13.3 reshape.357
  1369.1 14.1 %copy.23 = f32[1,4096,1024]{2,1,0:T(8,128)} copy(bf16[1,4096,1024]{2,0,1:T(2,128)(2,1)} %bitcast.209) | data formatting | bytes 25165824
  (89 shorter events, 115.0 us)
Async XLA Ops:
  6.5 7.5 copy-start.5
  6.5 58.6 %all-gather.5.cloned.1.call-start = ((), (), s32[]{:S(2)}) async-start(), calls=%async_computation.4 | async-start | bytes 9437184 | tf_op jit(solution)/shard_map/all_gather | solution.py:37
  290.1 5.3 copy-start.15
  290.1 98.8 %all-to-all-start = ((bf16[8,2,262144]{2,1,0:T(2,128)(2,1)}), bf16[8,2,262144]{2,1,0:T(2,128)(2,1)}, u32[]{:S(2)}, u32[]{:S(2)}) async-start(bf16[8,2,262144]{2,1,0:T(2,128)(2,1)} %reshape.350), calls=%async_computation | async-start | bytes 16777216 | tf_op jit(solution)/shard_map/all_to_all | solution.py:24
  295.4 178.4 %all-gather.7.cloned.1.call-start = ((), (), s32[]{:S(2)}) async-start(), calls=%async_computation.5 | async-start | bytes 9437184 | tf_op jit(solution)/shard_map/all_gather | solution.py:43
  416.5 8.1 copy-start
  424.6 0.9 copy-start.12
  424.6 0.9 copy-start.13
  424.9 2.1 copy-start.17
  565.7 5.3 copy-start.16
  565.7 98.9 %all-to-all-start.1 = ((bf16[8,2,262144]{2,1,0:T(2,128)(2,1)}), bf16[8,2,262144]{2,1,0:T(2,128)(2,1)}, u32[]{:S(2)}, u32[]{:S(2)}) async-start(bf16[8,2,262144]{2,1,0:T(2,128)(2,1)} %reshape.352), calls=%async_computation.1 | async-start | bytes 16777216 | tf_op jit(solution)/shard_map/all_to_all | solution.py:24
  570.9 181.9 %all-gather.9.cloned.1.call-start = ((), (), s32[]{:S(2)}) async-start(), calls=%async_computation.6 | async-start | bytes 9437184 | tf_op jit(solution)/shard_map/all_gather | solution.py:37
  701.2 3.4 copy-start.9
  701.2 3.4 copy-start.10
  703.3 1.4 copy-start.1
  703.3 49.5 %copy-start.6 = (bf16[1,1024,3,2,64]{1,4,3,2,0:T(8,128)(2,1)S(1)}, bf16[1,1024,3,2,64]{1,4,3,2,0:T(8,128)(2,1)}, u32[]{:S(2)}) copy-start(bf16[1,1024,3,2,64]{1,4,3,2,0:T(8,128)(2,1)} %get-tuple-element.9) | copy-start | bytes 2359300
  706.1 459.0 %all-gather.11.cloned.1.call-start = ((), (), s32[]{:S(2)}) async-start(), calls=%async_computation.7 | async-start | bytes 9437184 | tf_op jit(solution)/shard_map/all_gather | solution.py:43
  1104.2 9.4 copy-start.2
  1104.2 9.4 copy-start.11
  1113.6 3.2 copy-start.7
  1113.6 3.2 copy-start.8
  1115.5 1.3 copy-start.3
  1115.5 49.6 %copy-start.18 = (f32[1,512]{1,0:T(1,128)S(1)}, f32[1,512]{1,0:T(1,128)}, u32[]{:S(2)}) copy-start(f32[1,512]{1,0:T(1,128)} %get-tuple-element.23) | copy-start | bytes 6148
  1115.5 49.6 %copy-start.19 = (bf16[2,512,1024]{2,1,0:T(8,128)(2,1)S(1)}, bf16[2,512,1024]{2,1,0:T(8,128)(2,1)}, u32[]{:S(2)}) copy-start(bf16[2,512,1024]{2,1,0:T(8,128)(2,1)} %param.16) | copy-start | bytes 6291460
  1383.2 9.4 copy-start.4
  1383.2 9.4 copy-start.14
Sparse Core Ops, SparseCore 0:
  14.1 50.9 all-gather.4
  427.2 46.5 all-gather.6
  706.2 46.5 all-gather.8
  1118.4 46.6 all-gather.10
where the time goes:
time: 1410 us; the launch traced here: 1400 us
  waiting for transfers between devices  376 us (27%)
  local copies, waits for them, and re-layouts  306 us (22%)
  other arithmetic  254 us (18%)
  matrix products  244 us (17%)
  blocking collectives  199 us (14%)
    all_to_all x2, blocking collectives, reduce_rows(): lax.all_to_all(partial.astype(jnp.bfloat16), 'tp', 1, 0, tiled=True)  199 us
    unnamed x4, other arithmetic  198 us
    all_to_all x2, waiting for transfers between devices, reduce_rows(): lax.all_to_all(partial.astype(jnp.bfloat16), 'tp', 1, 0, tiled=True)  186 us
    unnamed x53, local copies, waits for them, and re-layouts  157 us
    convert_element_type x4, local copies, waits for them, and re-layouts, reduce_rows(): partial.astype(jnp.bfloat16)  145 us
    sub x2, matrix products, attention(): attn_prob = jax.nn.softmax(scores, axis=-1).astype(jnp.bfloat16)  108 us
    all_gather x2, waiting for transfers between devices, local_layers(): full_rows = lax.all_gather(normed, 'tp', axis=1, tiled=True)  96.7 us
    all_gather x2, waiting for transfers between devices, local_layers(): full_rows2 = lax.all_gather(normed2, 'tp', axis=1, tiled=True)  93 us
  transfers between devices with their start and end apart: 6, of which 6 were waited for; matrix products, arithmetic and copies ran while one was open for 0% of the time, Pallas kernels for 0%

commit v1 on v0

v1 whole, which is shorter than its diff:
```python
import functools
import jax
import jax.numpy as jnp
from jax import lax
from jax.experimental import pallas as pl
from jax.experimental.pallas import tpu as pltpu
from jax.sharding import PartitionSpec as P

LN_EPS = 1e-5
LOG2E = 1.4426950408889634
NT = (((1,), (1,)), ((), ()))
VMEM_LIMIT = 60 * 2**20


def layer_norm(rows, gain, shift):
    row_mean = jnp.mean(rows, axis=-1, keepdims=True)
    centred = rows - row_mean
    row_var = jnp.mean(centred * centred, axis=-1, keepdims=True)
    return (centred * lax.rsqrt(row_var + LN_EPS) * gain + shift).astype(jnp.bfloat16)


def whole():
    return pl.BlockSpec(memory_space=pltpu.VMEM)


def norm_kernel(rows_ref, norms_ref, out_ref):
    out_ref[...] = layer_norm(rows_ref[...].astype(jnp.float32), norms_ref[0:1, :], norms_ref[1:2, :])


def norm_rows(rows, norms):
    return pl.pallas_call(
        norm_kernel,
        out_shape=jax.ShapeDtypeStruct(rows.shape, jnp.bfloat16),
        in_specs=[whole()] * 2,
        out_specs=whole(),
        cost_estimate=pl.CostEstimate(flops=10 * rows.size, bytes_accessed=4 * rows.size, transcendentals=0),
        name='norm_rows',
    )(rows, norms)


def attn_kernel(head_dim, qt, kc, x_ref, wqk_ref, wvt_ref, o_ref, q_s, k_s, vt_s, s_s, acc_s):
    seq = x_ref.shape[0]
    pair = 2 * head_dim
    rows = 512
    n_heads = 2
    scale = head_dim ** -0.5 * LOG2E
    vt_s[:, head_dim:, :] = jnp.ones((n_heads, vt_s.shape[1] - head_dim, seq), jnp.bfloat16)

    @pl.loop(0, seq // rows)
    def _(i):
        at = pl.ds(pl.multiple_of(i * rows, rows), rows)
        xr = x_ref[at, :]
        qk = jnp.dot(xr, wqk_ref[...], preferred_element_type=jnp.float32)
        q_s[at, :] = qk[:, :pair].astype(jnp.bfloat16)
        k_s[at, :] = qk[:, pair:].astype(jnp.bfloat16)
        vt = lax.dot_general(wvt_ref[...], xr, NT, preferred_element_type=jnp.float32).astype(jnp.bfloat16)
        for h in range(n_heads):
            vt_s[h, :head_dim, at] = vt[h * head_dim:(h + 1) * head_dim]

    n_tiles = seq // qt
    n_chunks = seq // kc

    def masked_q(j):
        q = q_s[pl.ds(pl.multiple_of(j * qt, qt), qt), :]
        lane = lax.broadcasted_iota(jnp.int32, q.shape, 1)
        zero = jnp.zeros_like(q)
        return jnp.concatenate([jnp.where(lane < head_dim, q, zero), jnp.where(lane >= head_dim, q, zero)], axis=0)

    def scores(c, qm):
        return lax.dot_general(k_s[c * kc:(c + 1) * kc, :], qm, NT, preferred_element_type=jnp.float32)

    def fold(s):
        return jnp.max(s.reshape(kc // 8, 8, s.shape[1]), axis=0)

    qm0 = masked_q(0)
    mx = jnp.full((8, 2 * qt), -jnp.inf, jnp.float32)
    for c in range(n_chunks):
        s = scores(c, qm0)
        s_s[0, c * kc:(c + 1) * kc, :] = s
        mx = jnp.maximum(mx, fold(s))
    m0 = jnp.max(mx, axis=0, keepdims=True) * scale

    def tile(j, m):
        slot = 0
        qm = masked_q(j)
        mx = jnp.full((8, 2 * qt), -jnp.inf, jnp.float32)
        for c in range(n_chunks):
            at = slice(c * kc, (c + 1) * kc)
            s = scores(c, qm)
            s_s[0, at, :] = s
            mx = jnp.maximum(mx, fold(s))
        m = jnp.max(mx, axis=0, keepdims=True) * scale
        for c in range(n_chunks):
            at = slice(c * kc, (c + 1) * kc)
            p = jnp.exp2(s_s[slot, at, :] * scale - m).astype(jnp.bfloat16)
            for h in range(n_heads):
                part = jnp.dot(vt_s[h, :, at], p[:, h * qt:(h + 1) * qt], preferred_element_type=jnp.float32)
                if c == 0:
                    acc_s[h] = part
                else:
                    acc_s[h] += part
        ots = []
        for h in range(n_heads):
            acc = acc_s[h]
            ots.append(acc[:head_dim] / acc[head_dim:head_dim + 1])
        ot = jnp.concatenate(ots, axis=0)
        o_ref[pl.ds(pl.multiple_of(j * qt, qt), qt), :] = ot.T.astype(jnp.bfloat16)
        return jnp.max(mx, axis=0, keepdims=True) * scale

    lax.fori_loop(0, n_tiles, tile, m0)

def attn(x, wqk, wvt, head_dim, qt=256, kc=512):
    seq = x.shape[0]
    return pl.pallas_call(
        functools.partial(attn_kernel, head_dim, qt, kc),
        out_shape=jax.ShapeDtypeStruct((seq, 2 * head_dim), jnp.bfloat16),
        in_specs=[pl.BlockSpec(memory_space=pltpu.VMEM)] * 3,
        out_specs=pl.BlockSpec(memory_space=pltpu.VMEM),
        scratch_shapes=[
            pltpu.VMEM((seq, 2 * head_dim), jnp.bfloat16),
            pltpu.VMEM((seq, 2 * head_dim), jnp.bfloat16),
            pltpu.VMEM((2, head_dim + 16, seq), jnp.bfloat16),
            pltpu.VMEM((2, seq, 2 * qt), jnp.float32),
            pltpu.VMEM((2, head_dim + 16, qt), jnp.float32),
        ],
        compiler_params=pltpu.CompilerParams(vmem_limit_bytes=60 * 2**20),
        cost_estimate=pl.CostEstimate(flops=12 * 10**9, bytes_accessed=10 * 2**20, transcendentals=2 * seq * seq),
        name="attn",
    )(x, wqk, wvt)


def mlp_kernel(layer, last, o_ref, res_ref, norms_ref, b_out_ref, b_down_ref, w_out_ref, w_up_ref, b_up_ref, w_down_ref, r_ref, h_ref, h2_s):
    step = pl.program_id(0)
    base = 4 * layer

    @pl.when(step == 0)
    def _():
        heads = jnp.concatenate([o_ref[i] for i in range(o_ref.shape[0])], axis=1)
        attn_out = jnp.dot(heads, w_out_ref[...], preferred_element_type=jnp.float32)
        r = res_ref[...].astype(jnp.float32) + attn_out + b_out_ref[layer:layer + 1, :]
        r_ref[...] = r
        h2_s[...] = layer_norm(r, norms_ref[base + 2:base + 3, :], norms_ref[base + 3:base + 4, :])

    hidden = jnp.dot(h2_s[...], w_up_ref[...], preferred_element_type=jnp.float32) + b_up_ref[...]
    gelu_out = jax.nn.gelu(hidden, approximate=True).astype(jnp.bfloat16)
    r_ref[...] += jnp.dot(gelu_out, w_down_ref[...], preferred_element_type=jnp.float32)

    @pl.when(step == pl.num_programs(0) - 1)
    def _():
        r = r_ref[...] + b_down_ref[layer:layer + 1, :]
        if last:
            h_ref[...] = r.astype(jnp.bfloat16)
        else:
            r_ref[...] = r
            h_ref[...] = layer_norm(r, norms_ref[base + 4:base + 5, :], norms_ref[base + 5:base + 6, :])


def mlp(layer, last, o, res, norms, b_out, b_down, w_out, w_up, b_up, w_down):
    n, width, ff = w_up.shape
    rows = res.shape[0]

    def whole_block(a):
        return pl.BlockSpec(a.shape, lambda i: (0,) * a.ndim)

    return pl.pallas_call(
        functools.partial(mlp_kernel, layer, last),
        grid=(n,),
        out_shape=(jax.ShapeDtypeStruct((rows, width), jnp.float32), jax.ShapeDtypeStruct((rows, width), jnp.bfloat16)),
        in_specs=[whole_block(o), whole_block(res), whole_block(norms), whole_block(b_out), whole_block(b_down), whole_block(w_out),
                  pl.BlockSpec((None, width, ff), lambda i: (i, 0, 0)),
                  pl.BlockSpec((None, None, 1, ff), lambda i: (i, layer, 0, 0)),
                  pl.BlockSpec((None, ff, width), lambda i: (i, 0, 0))],
        out_specs=(pl.BlockSpec((rows, width), lambda i: (0, 0)), pl.BlockSpec((rows, width), lambda i: (0, 0))),
        scratch_shapes=[pltpu.VMEM((rows, width), jnp.bfloat16)],
        compiler_params=pltpu.CompilerParams(dimension_semantics=('arbitrary',), vmem_limit_bytes=VMEM_LIMIT),
        cost_estimate=pl.CostEstimate(flops=4 * rows * width * ff * n, bytes_accessed=4 * n * width * ff, transcendentals=rows * n * ff),
        name='mlp',
    )(o, res, norms, b_out, b_down, w_out, w_up, b_up, w_down)


def solution(mesh):
    group_size = mesh.shape['tp']

    def local_layers(hidden_in, norms, w_qkv, w_out, b_out, w_up, b_up, w_down, b_down):
        n_layers, width, slots, heads_loc, head_dim = w_qkv.shape
        rows = hidden_in.shape[1]
        pair = heads_loc * head_dim
        norms = norms.reshape(n_layers * 4, width)
        residual = hidden_in[0]
        normed = norm_rows(residual, norms)
        b_up_all = lax.all_gather(b_up.reshape(n_layers, 1, -1), 'tp')
        for layer in range(n_layers):
            w_l = w_qkv[layer].reshape(width, slots * pair)
            wqk, wvt = w_l[:, :2 * pair], w_l[:, 2 * pair:].T
            x = lax.all_gather(normed, 'tp', axis=0, tiled=True)
            x, w_out_l, w_up_l, w_down_l = lax.optimization_barrier((x, w_out[layer].reshape(pair, width), w_up[layer], w_down[layer]))
            w_out_all = lax.all_gather(w_out_l, 'tp', axis=0, tiled=True)
            w_up_all = lax.all_gather(w_up_l, 'tp')
            w_down_all = lax.all_gather(w_down_l, 'tp')
            o = attn(x, wqk, wvt, head_dim)
            o = lax.all_to_all(o.reshape(group_size, rows, pair), 'tp', 0, 0)
            residual, normed = mlp(layer, layer == n_layers - 1, o, residual, norms, b_out, b_down, w_out_all, w_up_all, b_up_all, w_down_all)
        return normed[None]

    in_specs = (P('dp', 'tp', None), P(), P(None, None, None, 'tp', None), P(None, 'tp', None, None), P(), P(None, None, 'tp'), P(None, 'tp'), P(None, 'tp', None), P())
    return jax.shard_map(local_layers, mesh=mesh, in_specs=in_specs, out_specs=P('dp', 'tp', None), check_vma=False)
```

time: 1410 us -> 408 us (0.29)
  local copies, waits for them, and re-layouts: 306 us -> 10.4 us
  other arithmetic: 254 us -> 0 us
  matrix products: 244 us -> 0 us
  waiting for transfers between devices: 376 us -> 177 us
  Pallas kernels: 0 us -> 153 us
  blocking collectives: 199 us -> 48.4 us
    unnamed x4 -> x0, other arithmetic: 198 us -> none
    all_to_all x2 -> x1, waiting for transfers between devices: 186 us -> 0.01 us  [local_layers(): o = lax.all_to_all(o.reshape(group_size, rows, pair), 'tp', 0, 0)]
    all_to_all x2 -> x1, blocking collectives: 199 us -> 22.5 us  [local_layers(): o = lax.all_to_all(o.reshape(group_size, rows, pair), 'tp', 0, 0)]
    unnamed x53 -> x12, local copies, waits for them, and re-layouts: 157 us -> 0.88 us
    pallas_call x0 -> x5, Pallas kernels: none -> 153 us  [the longest x2 112 us: attn(): pl.pallas_call(functools.partial(attn_kernel, head_dim, qt, kc), out_shap...]
    convert_element_type x4 -> x0, local copies, waits for them, and re-layouts: 145 us -> none  [reduce_rows(): partial.astype(jnp.bfloat16)]
    dot_general x6 -> x0, matrix products: 124 us -> none  [the longest x2 85.8 us: attention(): jnp.einsum('bhqk,bkhe->bqhe', attn_prob, qkv_rows[:, :, 2], preferred_ele...]
    sub x2 -> x0, matrix products: 108 us -> none  [attention(): attn_prob = jax.nn.softmax(scores, axis=-1).astype(jnp.bfloat16)]
  transfers between devices with their start and end apart: 6 -> 9, of which waited for: 6 -> 4; matrix products, arithmetic and copies ran while one was open for 0% -> 2% of each run, Pallas kernels for 0% -> 28%
where the time goes in v1:
time: 408 us; the launch traced here: 407 us
  waiting for transfers between devices  177 us (43%)
  Pallas kernels  153 us (38%)
  blocking collectives  48.4 us (12%)
  between operations  13.6 us (3%)
  local copies, waits for them, and re-layouts  10.4 us (3%)
  starting transfers between devices  4.43 us (1%)
    pallas_call x2, Pallas kernels, attn(): pl.pallas_call(functools.partial(attn_kernel, head_dim, qt, kc), out_shap...  112 us
    all_gather x2, waiting for transfers between devices, local_layers(): x = lax.all_gather(normed, 'tp', axis=0, tiled=True)  93.1 us
    all_gather x2, waiting for transfers between devices, local_layers(): w_down_all = lax.all_gather(w_down_l, 'tp')  81.3 us
    pallas_call x2, Pallas kernels, mlp(): pl.pallas_call(functools.partial(mlp_kernel, layer, last), grid=(n,), out...  37.8 us
    all_gather x1, blocking collectives, local_layers(): b_up_all = lax.all_gather(b_up.reshape(n_layers, 1, -1), 'tp')  25.9 us
    all_to_all x1, blocking collectives, local_layers(): o = lax.all_to_all(o.reshape(group_size, rows, pair), 'tp', 0, 0)  22.5 us
  transfers between devices with their start and end apart: 9, of which 4 were waited for; matrix products, arithmetic and copies ran while one was open for 2% of the time, Pallas kernels for 28%

profile of v1, /device:TPU:81, one launch (start us, length us, event | category | flops | bytes accessed | tf_op | source)
XLA Modules:
  0.0 406.9 jit_solution(6528285458361135643)
XLA Ops:
  6.6 1.4 reshape.9.norms_ref
  8.0 3.1 norm_rows.1
  11.1 0.1 all-gather.17.cloned.1.call-start
  11.2 0.8 fusion.1
  12.0 1.5 slice_bitcast_fusion.1
  13.5 0.9 copy-done.1
  14.4 1.5 slice_bitcast_fusion
  15.9 46.4 %all-gather.15.cloned.1.call-done.x_ref = bf16[4096,1024]{1,0:T(8,128)(2,1)} async-done(((bf16[512,1024]{1,0:T(8,128)(2,1)}), bf16[4096,1024]{1,0:T(8,128)(2,1)}) %all-gather.15.cloned.1.call-update) | async-done | bytes 8388624 | tf_op jit(solution)/shard_map/all_gather | solution.py:195
  62.3 0.1 all-gather.23.cloned.1.call-start
  62.4 0.7 all-gather.23.cloned.1.call-update
  63.1 0.1 all-gather.25.cloned.1.call-start
  63.2 0.6 all-gather.25.cloned.1.call-update
  63.8 0.1 fusion
  63.9 1.0 copy.12.wqk_ref
  65.0 0.7 slice_bitcast_fusion.5.wvt_ref
  65.7 56.0 %attn.2 = bf16[4096,128]{1,0:T(8,128)(2,1)} custom-call(bf16[4096,1024]{1,0:T(8,128)(2,1)} %all-gather.15.cloned.1.call-done.x_ref, bf16[1024,256]{1,0:T(8,128)(2,1)} %copy.12.wqk_ref, bf16[128,1024]{1,0:T(8,128)(2,1)} %slice_bitcast_fusion.5.wvt_ref), custom_call_target="tpu_custom_call" | custom-call | flops 12000000000 | bytes 10485760 | tf_op jit(solution)/shard_map/attn/pallas_call | solution.py:114
  121.7 3.9 all-to-all-start
  125.6 25.9 %all-gather.5 = f32[8,2,512]{2,1,0:T(2,128)S(1)} all-gather(f32[1,2,512]{2,1,0:T(2,128)S(1)} %bitcast.35), channel_id=3, replica_groups=mesh['dp'=4,'tp'=8] {'tp'}, dimensions={0}, use_global_device_ids=true | all-gather | bytes 36864 | tf_op jit(solution)/shard_map/all_gather | solution.py:191
  151.5 0.6 reshape.13.b_up_ref
  152.1 36.2 %all-gather.25.cloned.1.call-done = bf16[4096,1024]{1,0:T(8,128)(2,1)} async-done(((bf16[512,1024]{1,0:T(8,128)(2,1)}), bf16[4096,1024]{1,0:T(8,128)(2,1)}) %all-gather.25.cloned.1.call-update) | async-done | bytes 8388624 | tf_op jit(solution)/shard_map/all_gather | solution.py:199
  188.3 19.1 %mlp.2 = (f32[512,1024]{1,0:T(8,128)}, bf16[512,1024]{1,0:T(8,128)(2,1)}) custom-call(bf16[8,512,128]{2,1,0:T(8,128)(2,1)} %copy-done.3, bf16[512,1024]{1,0:T(8,128)(2,1)} %bitcast.30, f32[8,1024]{1,0:T(8,128)} %reshape.9.norms_ref, f32[2,1024]{1,0:T(2,128)} %b_out_ref.3, f32[2,1024]{1,0:T(2,128)} %b_down_ref.3, ...), custom_call_target="tpu_custom_call" | custom-call | flops 8589934592 | bytes 16777216 | tf_op jit(solution)/shard_map/mlp/pallas_call | solution.py:165
  207.4 0.1 all-gather.21.cloned.1.call-start
  207.5 46.7 %all-gather.19.cloned.1.call-done.x_ref = bf16[4096,1024]{1,0:T(8,128)(2,1)} async-done(((bf16[512,1024]{1,0:T(8,128)(2,1)}), bf16[4096,1024]{1,0:T(8,128)(2,1)}) %all-gather.19.cloned.1.call-update) | async-done | bytes 8388624 | tf_op jit(solution)/shard_map/all_gather | solution.py:195
  254.3 0.7 all-gather.27.cloned.1.call-update
  255.1 0.2 all-gather.29.cloned.1.call-start
  255.3 0.6 all-gather.29.cloned.1.call-update
  255.9 1.0 copy.13.wqk_ref
  257.0 0.7 slice_bitcast_fusion.4.wvt_ref
  257.7 56.0 %attn.3 = bf16[4096,128]{1,0:T(8,128)(2,1)} custom-call(bf16[4096,1024]{1,0:T(8,128)(2,1)} %all-gather.19.cloned.1.call-done.x_ref, bf16[1024,256]{1,0:T(8,128)(2,1)} %copy.13.wqk_ref, bf16[128,1024]{1,0:T(8,128)(2,1)} %slice_bitcast_fusion.4.wvt_ref), custom_call_target="tpu_custom_call" | custom-call | flops 12000000000 | bytes 10485760 | tf_op jit(solution)/shard_map/attn/pallas_call | solution.py:114
  313.7 22.5 %all_to_all.10.o_ref = bf16[8,512,128]{2,1,0:T(8,128)(2,1)} all-to-all(bf16[8,512,128]{2,1,0:T(8,128)(2,1)} %bitcast.32), channel_id=1, replica_groups=mesh['dp'=4,'tp'=8] {'tp'}, dimensions={0} | all-to-all | bytes 2097152 | tf_op jit(solution)/shard_map/all_to_all | solution.py:201
  336.2 45.1 %all-gather.29.cloned.1.call-done = bf16[4096,1024]{1,0:T(8,128)(2,1)} async-done(((bf16[512,1024]{1,0:T(8,128)(2,1)}), bf16[4096,1024]{1,0:T(8,128)(2,1)}) %all-gather.29.cloned.1.call-update) | async-done | bytes 8388624 | tf_op jit(solution)/shard_map/all_gather | solution.py:199
  381.3 18.7 %mlp.3 = (f32[512,1024]{1,0:T(8,128)}, bf16[512,1024]{1,0:T(8,128)(2,1)}) custom-call(bf16[8,512,128]{2,1,0:T(8,128)(2,1)} %all_to_all.10.o_ref, f32[512,1024]{1,0:T(8,128)} %get-tuple-element.22.res_ref, f32[8,1024]{1,0:T(8,128)} %reshape.9.norms_ref, f32[2,1024]{1,0:T(2,128)} %b_out_ref.3, f32[2,1024]{1,0:T(2,128)} %b_down_ref.3, ...), custom_call_target="tpu_custom_call" | custom-call | flops 8589934592 | bytes 16777216 | tf_op jit(solution)/shard_map/mlp/pallas_call | solution.py:165
  (25 shorter events, 0.4 us)
Async XLA Ops:
  6.5 4.7 %copy-start.4 = (bf16[2,2,64,1024]{3,2,1,0:T(8,128)(2,1)S(1)}, bf16[2,2,64,1024]{3,2,1,0:T(8,128)(2,1)}, u32[]{:S(2)}) copy-start(bf16[2,2,64,1024]{3,2,1,0:T(8,128)(2,1)} %param.12) | copy-start | bytes 1572868
  6.5 55.7 %all-gather.15.cloned.1.call-start = ((), (), s32[]{:S(2)}) async-start(), calls=%async_computation.2 | async-start | bytes 9437184 | tf_op jit(solution)/shard_map/all_gather | solution.py:195
  8.0 4.0 copy-start
  11.1 141.0 %all-gather.17.cloned.1.call-start = ((), (), s32[]{:S(2)}) async-start(), calls=%async_computation.3 | async-start | bytes 2359296 | tf_op jit(solution)/shard_map/all_gather | solution.py:197
  12.0 2.3 copy-start.1
  15.9 47.9 %copy-start.2 = (bf16[2,1024,3,2,64]{1,4,3,2,0:T(8,128)(2,1)S(1)}, bf16[2,1024,3,2,64]{1,4,3,2,0:T(8,128)(2,1)}, u32[]{:S(2)}) copy-start(bf16[2,1024,3,2,64]{1,4,3,2,0:T(8,128)(2,1)} %param.11) | copy-start | bytes 4718596
  62.3 89.8 %all-gather.23.cloned.1.call-start = ((), (), s32[]{:S(2)}) async-start(), calls=%async_computation.6 | async-start | bytes 9437184 | tf_op jit(solution)/shard_map/all_gather | solution.py:198
  63.1 125.2 %all-gather.25.cloned.1.call-start = ((), (), s32[]{:S(2)}) async-start(), calls=%async_computation.7 | async-start | bytes 9437184 | tf_op jit(solution)/shard_map/all_gather | solution.py:199
  121.7 3.9 copy-start.5
  121.7 30.4 %all-to-all-start = ((bf16[8,512,128]{2,1,0:T(8,128)(2,1)}), bf16[8,512,128]{2,1,0:T(8,128)(2,1)S(1)}, u32[]{:S(2)}, u32[]{:S(2)}) async-start(bf16[8,512,128]{2,1,0:T(8,128)(2,1)} %bitcast.31), calls=%async_computation | async-start | bytes 2097152 | tf_op jit(solution)/shard_map/all_to_all | solution.py:201
  125.6 128.6 %all-gather.19.cloned.1.call-start = ((), (), s32[]{:S(2)}) async-start(), calls=%async_computation.4 | async-start | bytes 9437184 | tf_op jit(solution)/shard_map/all_gather | solution.py:195
  152.1 36.2 %copy-start.3 = (bf16[8,512,128]{2,1,0:T(8,128)(2,1)}, bf16[8,512,128]{2,1,0:T(8,128)(2,1)S(1)}, u32[]{:S(2)}) copy-start(bf16[8,512,128]{2,1,0:T(8,128)(2,1)S(1)} %all-to-all-done.o_ref) | copy-start | bytes 3145732
  207.4 128.8 %all-gather.21.cloned.1.call-start = ((), (), s32[]{:S(2)}) async-start(), calls=%async_computation.5 | async-start | bytes 2359296 | tf_op jit(solution)/shard_map/all_gather | solution.py:197
  254.3 81.9 %all-gather.27.cloned.1.call-start = ((), (), s32[]{:S(2)}) async-start(), calls=%async_computation.8 | async-start | bytes 9437184 | tf_op jit(solution)/shard_map/all_gather | solution.py:198
  255.1 126.3 %all-gather.29.cloned.1.call-start = ((), (), s32[]{:S(2)}) async-start(), calls=%async_computation.9 | async-start | bytes 9437184 | tf_op jit(solution)/shard_map/all_gather | solution.py:199
Sparse Core Ops, SparseCore 0:
  11.3 50.9 all-gather.14
  63.9 22.1 all-gather.16
  87.7 52.1 all-gather.22
  141.4 46.8 all-gather.24
  207.6 46.6 all-gather.18
  255.7 22.1 all-gather.20
  279.5 53.1 all-gather.26
  334.4 46.9 all-gather.28

commit v2 on v0

v2 whole, which is shorter than its diff:
```python
import functools
import jax
import jax.numpy as jnp
from jax import lax
from jax.experimental import pallas as pl
from jax.experimental.pallas import tpu as pltpu
from jax.sharding import PartitionSpec as P

MESH = pl.DeviceIdType.MESH
LN_EPS = 1e-5
LOG2E = 1.4426950408889634
NT = (((1,), (1,)), ((), ()))
VMEM_LIMIT = 63 * 2**20

ME, SIB, LEFT, RIGHT, OPP, SLEFT, SRIGHT, SOPP = range(8)
INVERSE = {SIB: SIB, LEFT: RIGHT, RIGHT: LEFT, OPP: OPP, SLEFT: SRIGHT, SRIGHT: SLEFT, SOPP: SOPP}
ACROSS = {ME: SIB, LEFT: SLEFT, RIGHT: SRIGHT, OPP: SOPP}
ORDER = [OPP, SOPP, LEFT, SLEFT, RIGHT, SRIGHT, SIB, ME]
PLACE = {rel: i for i, rel in enumerate(ORDER)}
PIECES = 4

Z_CHUNKS = ['zu0', 'zu1', 'zd0', 'zd1']
X_CHUNKS = Z_CHUNKS + ['cu', 'cd', 'co']
TO_RIGHT = ['zu0', 'zd0', 'co', 'zu1', 'zd1', 'cu', 'cd']
TO_LEFT = ['zu1', 'zd1', 'cu', 'zu0', 'zd0', 'cd', 'co']
RELAY_RIGHT = ['zu0', 'zd0', 'co']
RELAY_LEFT = ['zu1', 'zd1', 'cu', 'cd']


def layer_norm(rows, gain, shift):
    row_mean = jnp.mean(rows, axis=-1, keepdims=True)
    centred = rows - row_mean
    row_var = jnp.mean(centred * centred, axis=-1, keepdims=True)
    return (centred * lax.rsqrt(row_var + LN_EPS) * gain + shift).astype(jnp.bfloat16)


def whole():
    return pl.BlockSpec(memory_space=pltpu.VMEM)


def norm_kernel(rows_ref, norms_ref, out_ref):
    out_ref[...] = layer_norm(rows_ref[...].astype(jnp.float32), norms_ref[0:1, :], norms_ref[1:2, :])


def norm_rows(rows, norms):
    return pl.pallas_call(
        norm_kernel,
        out_shape=jax.ShapeDtypeStruct(rows.shape, jnp.bfloat16),
        in_specs=[whole()] * 2,
        out_specs=whole(),
        cost_estimate=pl.CostEstimate(flops=10 * rows.size, bytes_accessed=4 * rows.size, transcendentals=0),
        name='norm_rows',
    )(rows, norms)


def message_keys():
    keys = []
    for p in range(PIECES):
        keys += [('xr', p), ('xl', p), ('xs', ME, p)]
        keys += [('xs', rel, p) for rel in (LEFT, RIGHT, OPP)]
        keys += [('xrr', p)] if p < PIECES // 2 else [('xll', p)]
    keys += [('wr', c) for c in X_CHUNKS] + [('wl', c) for c in X_CHUNKS]
    keys += [('wrr', c) for c in RELAY_RIGHT] + [('wll', c) for c in RELAY_LEFT]
    keys += [('ws', a) for a in ('u', 'd', 'o')]
    for rel in (LEFT, RIGHT, OPP):
        keys += [('wfx', rel, c) for c in X_CHUNKS]
        keys += [('wz', rel, c) for c in Z_CHUNKS] + [('wfz', rel, c) for c in Z_CHUNKS]
    keys += [('o', rel) for rel in INVERSE] + [('b', rel) for rel in INVERSE]
    return keys


KEYS = {key: i for i, key in enumerate(message_keys())}


def layer_kernel(layer, last, group_size, qt, kc, h_ref, res_ref, norms_ref, b_out_ref, b_down_ref, b_up_ref, wqk_ref, wvt_ref,
                 w_out_ref, w_up_ref, w_down_ref, r_ref, hn_ref,
                 x_v, wo_v, wu_v, wd_v, bu_v, q_s, k_s, vt_s, s_s, acc_s, o_loc, o_rcv, h2_s, send_sems, recv_sems, own_sems):
    rows, width = h_ref.shape
    ff = w_up_ref.shape[-1]
    seq = q_s.shape[0]
    pair = q_s.shape[1]
    n_heads = 2
    head_dim = pair // n_heads
    scale = head_dim ** -0.5 * LOG2E
    base = 4 * layer

    me = lax.axis_index('tp')
    chip, core = me // 2, me % 2
    n_chips = group_size // 2
    parity = lax.axis_index('dp') % 2
    partner = lax.axis_index('dp') + 1 - 2 * parity

    def at(step, flip):
        return {'tp': 2 * ((chip + step) % n_chips) + (1 - core if flip else core)}

    far = n_chips // 2
    device = {SIB: at(0, True), LEFT: at(n_chips - 1, False), RIGHT: at(1, False), OPP: at(far, False),
              SLEFT: at(n_chips - 1, True), SRIGHT: at(1, True), SOPP: at(far, True)}
    pair_device = {'dp': partner, 'tp': me}

    piece_rows = rows // PIECES
    up_z, down_z = width * 7 // 32, ff * 7 // 32

    def x_at(rel, p):
        ref = h_ref if rel == ME else x_v.at[rel]
        return ref.at[p * piece_rows:(p + 1) * piece_rows, :]

    def w_at(rel, c, par):
        if c == 'co':
            return wo_v.at[rel]
        if c == 'cu':
            return wu_v.at[rel, 4 * up_z:, :]
        if c == 'cd':
            return wd_v.at[rel, 4 * down_z:, :]
        i = int(c[2])
        if c[1] == 'u':
            return wu_v.at[rel, pl.ds(pl.multiple_of(par * (2 * up_z) + i * up_z, 16), up_z), :]
        return wd_v.at[rel, pl.ds(pl.multiple_of(par * (2 * down_z) + i * down_z, 16), down_z), :]

    def message(key, receiving=False):
        kind = key[0]
        here, there = parity, 1 - parity
        if kind == 'xr':
            src, dst, dev = x_at(ME, key[1]), x_at(LEFT, key[1]), device[RIGHT]
        elif kind == 'xl':
            src, dst, dev = x_at(ME, key[1]), x_at(RIGHT, key[1]), device[LEFT]
        elif kind == 'xrr':
            src, dst, dev = x_at(LEFT, key[1]), x_at(OPP, key[1]), device[RIGHT]
        elif kind == 'xll':
            src, dst, dev = x_at(RIGHT, key[1]), x_at(OPP, key[1]), device[LEFT]
        elif kind == 'xs':
            src, dst, dev = x_at(key[1], key[2]), x_at(ACROSS[key[1]], key[2]), device[SIB]
        elif kind == 'wr':
            src, dst, dev = w_at(ME, key[1], here), w_at(LEFT, key[1], here), device[RIGHT]
        elif kind == 'wl':
            src, dst, dev = w_at(ME, key[1], here), w_at(RIGHT, key[1], here), device[LEFT]
        elif kind == 'wrr':
            src, dst, dev = w_at(LEFT, key[1], here), w_at(OPP, key[1], here), device[RIGHT]
        elif kind == 'wll':
            src, dst, dev = w_at(RIGHT, key[1], here), w_at(OPP, key[1], here), device[LEFT]
        elif kind == 'ws':
            ref = {'u': wu_v, 'd': wd_v, 'o': wo_v}[key[1]]
            src, dst, dev = ref.at[ME], ref.at[SIB], device[SIB]
        elif kind == 'wfx':
            src, dst, dev = w_at(key[1], key[2], here), w_at(ACROSS[key[1]], key[2], here), device[SIB]
        elif kind == 'wz':
            par = there if receiving else here
            src, dst, dev = w_at(key[1], key[2], par), w_at(key[1], key[2], par), pair_device
        elif kind == 'wfz':
            src, dst, dev = w_at(key[1], key[2], there), w_at(ACROSS[key[1]], key[2], there), device[SIB]
        elif kind == 'o':
            src = o_loc.at[PLACE[key[1]] * rows:(PLACE[key[1]] + 1) * rows, :]
            dst, dev = o_rcv.at[INVERSE[key[1]]], device[key[1]]
        else:
            src, dst, dev = b_up_ref, bu_v.at[INVERSE[key[1]]], device[key[1]]
        i = KEYS[key]
        return pltpu.make_async_remote_copy(src_ref=src, dst_ref=dst, send_sem=send_sems.at[i], recv_sem=recv_sems.at[i],
                                            device_id=dev, device_id_type=MESH)

    def start(*key):
        message(key).start()

    def recv(*key):
        message(key, True).wait_recv()

    def own_copies():
        return [pltpu.make_async_copy(w_up_ref.at[layer], wu_v.at[ME], own_sems.at[0]),
                pltpu.make_async_copy(w_down_ref.at[layer], wd_v.at[ME], own_sems.at[1]),
                pltpu.make_async_copy(w_out_ref.at[layer], wo_v.at[ME], own_sems.at[2])]

    for copy in own_copies():
        copy.start()
    barrier = pltpu.get_barrier_semaphore()
    peers = list(device.values()) + [pair_device]
    for dev in peers:
        pl.semaphore_signal(barrier, inc=1, device_id=dev, device_id_type=MESH)
    pl.semaphore_wait(barrier, len(peers))

    right_order = list(range(PIECES))
    left_order = right_order[PIECES // 2:] + right_order[:PIECES // 2]
    for k in range(PIECES):
        start('xr', right_order[k])
        start('xl', left_order[k])
        start('xs', ME, k)
    for rel in INVERSE:
        start('b', rel)

    vt_s[:, head_dim:, :] = jnp.ones((n_heads, vt_s.shape[1] - head_dim, seq), jnp.bfloat16)

    def project(rel):
        place = slice(PLACE[rel] * rows, (PLACE[rel] + 1) * rows)
        xr = h_ref[...] if rel == ME else x_v[rel]
        qk = jnp.dot(xr, wqk_ref[...], preferred_element_type=jnp.float32)
        q_s[place, :] = qk[:, :pair].astype(jnp.bfloat16)
        k_s[place, :] = qk[:, pair:].astype(jnp.bfloat16)
        vt = lax.dot_general(wvt_ref[...], xr, NT, preferred_element_type=jnp.float32).astype(jnp.bfloat16)
        for h in range(n_heads):
            vt_s[h, :head_dim, place] = vt[h * head_dim:(h + 1) * head_dim]

    project(ME)
    for p in range(PIECES):
        recv('xs', ME, p)
    project(SIB)
    for k in range(PIECES):
        recv('xr', right_order[k])
        if k < PIECES // 2:
            start('xrr', right_order[k])
        start('xs', LEFT, right_order[k])
        recv('xl', left_order[k])
        if k < PIECES // 2:
            start('xll', left_order[k])
        start('xs', RIGHT, left_order[k])
        if k == PIECES // 2 - 1:
            for copy in own_copies():
                copy.wait()
            for i in range(2):
                start('wr', TO_RIGHT[i])
                start('wl', TO_LEFT[i])
            for a in ('u', 'd', 'o'):
                start('ws', a)
    project(LEFT)
    project(RIGHT)
    for rel in (LEFT, RIGHT):
        for p in range(PIECES):
            recv('xs', rel, p)
        project(ACROSS[rel])
    for k in range(PIECES // 2):
        recv('xrr', right_order[k])
        start('xs', OPP, right_order[k])
        recv('xll', left_order[k])
        start('xs', OPP, left_order[k])
    project(OPP)
    for p in range(PIECES):
        recv('xs', OPP, p)
    project(SOPP)

    def own(i):
        start('wr', TO_RIGHT[i])
        start('wl', TO_LEFT[i])

    def near(i):
        for kind, relay, rel, c, relayed in (('wr', 'wrr', LEFT, TO_RIGHT[i], RELAY_RIGHT), ('wl', 'wll', RIGHT, TO_LEFT[i], RELAY_LEFT)):
            recv(kind, c)
            if c in relayed:
                start(relay, c)
            if c in Z_CHUNKS:
                start('wz', rel, c)
            start('wfx', rel, c)

    def opposite(chunks):
        for c in chunks:
            recv('wrr' if c in RELAY_RIGHT else 'wll', c)
            if c in Z_CHUNKS:
                start('wz', OPP, c)
            start('wfx', OPP, c)

    def handed(rel, chunks):
        for c in chunks:
            recv('wz', rel, c)
            start('wfz', rel, c)

    ticks = {
        1: [lambda: own(2)],
        2: [lambda: near(0), lambda: own(3)],
        4: [lambda: near(1), lambda: own(4)],
        6: [lambda: near(2), lambda: own(5)],
        7: [lambda: handed(LEFT, ['zu0']), lambda: handed(RIGHT, ['zu1'])],
        8: [lambda: opposite(['zu0', 'zu1']), lambda: own(6)],
        9: [lambda: near(3)],
        10: [lambda: handed(LEFT, ['zd0']), lambda: handed(RIGHT, ['zd1'])],
        11: [lambda: opposite(['zd0', 'zd1'])],
        12: [lambda: near(4)],
        14: [lambda: opposite(['cu', 'co'])],
        15: [lambda: handed(OPP, ['zu0', 'zu1'])],
    }
    for i, rel in enumerate(ORDER[:-1]):
        ticks.setdefault(2 * i + 3, []).insert(0, lambda rel=rel: start('o', rel))

    n_tiles = seq // qt
    n_chunks = seq // kc

    def tile(j, carry):
        for when, actions in ticks.items():
            @pl.when(j == when)
            def _(actions=actions):
                for action in actions:
                    action()
        q = q_s[pl.ds(pl.multiple_of(j * qt, qt), qt), :]
        lane = lax.broadcasted_iota(jnp.int32, q.shape, 1)
        zero = jnp.zeros_like(q)
        qm = jnp.concatenate([jnp.where(lane < head_dim, q, zero), jnp.where(lane >= head_dim, q, zero)], axis=0)
        mx = jnp.full((8, n_heads * qt), -jnp.inf, jnp.float32)
        for c in range(n_chunks):
            keys = slice(c * kc, (c + 1) * kc)
            s = lax.dot_general(k_s[keys, :], qm, NT, preferred_element_type=jnp.float32)
            s_s[keys, :] = s
            mx = jnp.maximum(mx, jnp.max(s.reshape(kc // 8, 8, s.shape[1]), axis=0))
        m = jnp.max(mx, axis=0, keepdims=True) * scale
        for c in range(n_chunks):
            keys = slice(c * kc, (c + 1) * kc)
            p = jnp.exp2(s_s[keys, :] * scale - m).astype(jnp.bfloat16)
            for h in range(n_heads):
                part = jnp.dot(vt_s[h, :, keys], p[:, h * qt:(h + 1) * qt], preferred_element_type=jnp.float32)
                if c == 0:
                    acc_s[h] = part
                else:
                    acc_s[h] += part
        heads = []
        for h in range(n_heads):
            acc = acc_s[h]
            heads.append(acc[:head_dim] / acc[head_dim:head_dim + 1])
        o_loc[pl.ds(pl.multiple_of(j * qt, qt), qt), :] = jnp.concatenate(heads, axis=0).T.astype(jnp.bfloat16)
        return carry

    lax.fori_loop(0, n_tiles, tile, 0)

    near(5)
    near(6)
    opposite(['cd'])
    handed(LEFT, ['zu1'])
    handed(RIGHT, ['zu0'])
    recv('ws', 'o')
    for rel in (LEFT, RIGHT, OPP):
        recv('wfx', rel, 'co')
    for rel in INVERSE:
        recv('o', rel)
        recv('b', rel)
    bu_v[ME] = b_up_ref[...]
    o_rcv[ME] = o_loc[PLACE[ME] * rows:(PLACE[ME] + 1) * rows, :]
    heads = jnp.concatenate([o_rcv[rel] for rel in range(group_size)], axis=1)
    attn_out = jnp.dot(heads, wo_v[...].reshape(width, width), preferred_element_type=jnp.float32)
    r = res_ref[...].astype(jnp.float32) + attn_out + b_out_ref[layer:layer + 1, :]
    r_ref[...] = r
    h2_s[...] = layer_norm(r, norms_ref[base + 2:base + 3, :], norms_ref[base + 3:base + 4, :])

    def arrive_across(rel):
        for c in X_CHUNKS:
            if c != 'co':
                recv('wfx', rel, c)
        for c in Z_CHUNKS:
            recv('wfz', rel, c)

    def before(rel):
        if rel == SIB:
            recv('ws', 'u')
            recv('ws', 'd')
            handed(OPP, ['zd0', 'zd1'])
        elif rel == LEFT:
            handed(LEFT, ['zd1'])
            handed(RIGHT, ['zd0'])
        elif rel == SLEFT:
            arrive_across(LEFT)
        elif rel == SRIGHT:
            arrive_across(RIGHT)
        elif rel == SOPP:
            arrive_across(OPP)

    @pl.loop(0, group_size)
    def _(block):
        for rel in (SIB, LEFT, SLEFT, SRIGHT, SOPP):
            @pl.when(block == rel)
            def _(rel=rel):
                before(rel)
        hidden = jnp.dot(h2_s[...], wu_v[block], preferred_element_type=jnp.float32) + bu_v[block]
        gelu_out = jax.nn.gelu(hidden, approximate=True).astype(jnp.bfloat16)
        r_ref[...] += jnp.dot(gelu_out, wd_v[block], preferred_element_type=jnp.float32)

    r = r_ref[...] + b_down_ref[layer:layer + 1, :]
    if last:
        hn_ref[...] = r.astype(jnp.bfloat16)
    else:
        r_ref[...] = r
        hn_ref[...] = layer_norm(r, norms_ref[base + 4:base + 5, :], norms_ref[base + 5:base + 6, :])
    for key in KEYS:
        message(key).wait_send()


def run_layer(layer, last, group_size, head_dim, h, res, norms, b_out, b_down, b_up, wqk, wvt, w_out, w_up, w_down, qt=256, kc=512):
    rows, width = h.shape
    ff = w_up.shape[-1]
    seq = rows * group_size
    pair = 2 * head_dim
    anywhere = pl.BlockSpec(memory_space=pl.ANY)
    bf16, f32 = jnp.bfloat16, jnp.float32
    return pl.pallas_call(
        functools.partial(layer_kernel, layer, last, group_size, qt, kc),
        out_shape=(jax.ShapeDtypeStruct((rows, width), f32), jax.ShapeDtypeStruct((rows, width), bf16)),
        in_specs=[whole()] * 8 + [anywhere] * 3,
        out_specs=(whole(), whole()),
        scratch_shapes=[
            pltpu.VMEM((group_size, rows, width), bf16),
            pltpu.VMEM((group_size, pair, width), bf16),
            pltpu.VMEM((group_size, width, ff), bf16),
            pltpu.VMEM((group_size, ff, width), bf16),
            pltpu.VMEM((group_size, 1, ff), f32),
            pltpu.VMEM((seq, pair), bf16),
            pltpu.VMEM((seq, pair), bf16),
            pltpu.VMEM((2, head_dim + 16, seq), bf16),
            pltpu.VMEM((seq, 2 * qt), f32),
            pltpu.VMEM((2, head_dim + 16, qt), f32),
            pltpu.VMEM((seq, pair), bf16),
            pltpu.VMEM((group_size, rows, pair), bf16),
            pltpu.VMEM((rows, width), bf16),
            pltpu.SemaphoreType.DMA((len(KEYS),)),
            pltpu.SemaphoreType.DMA((len(KEYS),)),
            pltpu.SemaphoreType.DMA((3,)),
        ],
        compiler_params=pltpu.CompilerParams(collective_id=layer, has_side_effects=True, vmem_limit_bytes=VMEM_LIMIT),
        cost_estimate=pl.CostEstimate(flops=22 * 10**9, bytes_accessed=10 * 2**20, transcendentals=2 * seq * seq),
        name='layer',
    )(h, res, norms, b_out, b_down, b_up, wqk, wvt, w_out, w_up, w_down)


def solution(mesh):
    group_size = mesh.shape['tp']

    def local_layers(hidden_in, norms, w_qkv, w_out, b_out, w_up, b_up, w_down, b_down):
        n_layers, width, slots, heads_loc, head_dim = w_qkv.shape
        pair = heads_loc * head_dim
        norms = norms.reshape(n_layers * 4, width)
        w_out = w_out.reshape(n_layers, pair, width)
        residual = hidden_in[0]
        normed = norm_rows(residual, norms)
        for layer in range(n_layers):
            w_l = w_qkv[layer].reshape(width, slots * pair)
            wqk, wvt = w_l[:, :2 * pair], w_l[:, 2 * pair:].T
            residual, normed = run_layer(layer, layer == n_layers - 1, group_size, head_dim, normed, residual, norms, b_out, b_down,
                                         b_up[layer:layer + 1], wqk, wvt, w_out, w_up, w_down)
        return normed[None]

    in_specs = (P('dp', 'tp', None), P(), P(None, None, None, 'tp', None), P(None, 'tp', None, None), P(), P(None, None, 'tp'), P(None, 'tp'), P(None, 'tp', None), P())
    return jax.shard_map(local_layers, mesh=mesh, in_specs=in_specs, out_specs=P('dp', 'tp', None), check_vma=False)
```

time: 1410 us -> 267 us (0.19)
  waiting for transfers between devices: 376 us -> 0 us
  local copies, waits for them, and re-layouts: 306 us -> 8.74 us
  Pallas kernels: 0 us -> 258 us
  other arithmetic: 254 us -> 0 us
  matrix products: 244 us -> 0 us
  blocking collectives: 199 us -> 0 us
    pallas_call x0 -> x3, Pallas kernels: none -> 258 us  [the longest x2 255 us: run_layer(): pl.pallas_call(functools.partial(layer_kernel, layer, last, group_size, q...]
    all_to_all x2 -> x0, blocking collectives: 199 us -> none  [reduce_rows(): lax.all_to_all(partial.astype(jnp.bfloat16), 'tp', 1, 0, tiled=True)]
    unnamed x4 -> x0, other arithmetic: 198 us -> none
    all_gather x4 -> x0, waiting for transfers between devices: 190 us -> none  [the longest x2 96.7 us: local_layers(): full_rows = lax.all_gather(normed, 'tp', axis=1, tiled=True)]
    all_to_all x2 -> x0, waiting for transfers between devices: 186 us -> none  [reduce_rows(): lax.all_to_all(partial.astype(jnp.bfloat16), 'tp', 1, 0, tiled=True)]
    unnamed x53 -> x3, local copies, waits for them, and re-layouts: 157 us -> 2.27 us
    convert_element_type x4 -> x0, local copies, waits for them, and re-layouts: 145 us -> none  [reduce_rows(): partial.astype(jnp.bfloat16)]
    dot_general x6 -> x0, matrix products: 124 us -> none  [the longest x2 85.8 us: attention(): jnp.einsum('bhqk,bkhe->bqhe', attn_prob, qkv_rows[:, :, 2], preferred_ele...]
  transfers between devices with their start and end apart: 6 -> 0, of which waited for: 6 -> 0; matrix products, arithmetic and copies ran while one was open for 0% -> 0% of each run, Pallas kernels for 0% -> 0%
where the time goes in v2:
time: 267 us
  Pallas kernels  258 us (97%)
  local copies, waits for them, and re-layouts  8.74 us (3%)
    pallas_call x2, Pallas kernels, run_layer(): pl.pallas_call(functools.partial(layer_kernel, layer, last, group_size, q...  255 us

profile of v2, /device:TPU:81, one launch (start us, length us, event | category | flops | bytes accessed | tf_op | source)
XLA Modules:
  0.0 267.2 jit_solution(2022947107872746301)
XLA Ops:
  0.0 0.0 copy-start
  0.0 1.4 fusion.1
  1.4 1.4 reshape.6.norms_ref
  2.8 2.9 %norm_rows.1.h_ref = bf16[512,1024]{1,0:T(8,128)(2,1)} custom-call(bf16[512,1024]{1,0:T(8,128)(2,1)} %bitcast.13, f32[8,1024]{1,0:T(8,128)} %reshape.6.norms_ref), custom_call_target="tpu_custom_call" | custom-call | flops 5242880 | bytes 2097152 | tf_op jit(solution)/shard_map/norm_rows/pallas_call | solution.py:46
  5.7 0.0 copy-done
  5.7 0.1 fusion
  5.9 0.7 slice_bitcast_fusion.1.wvt_ref
  6.6 1.0 copy.10.wqk_ref
  7.6 0.7 slice_bitcast_fusion.wvt_ref
  8.4 1.0 copy.11.wqk_ref
  9.4 130.0 %layer.2 = (f32[512,1024]{1,0:T(8,128)}, bf16[512,1024]{1,0:T(8,128)(2,1)}) custom-call(bf16[512,1024]{1,0:T(8,128)(2,1)} %norm_rows.1.h_ref, bf16[512,1024]{1,0:T(8,128)(2,1)} %bitcast.14, f32[8,1024]{1,0:T(8,128)} %reshape.6.norms_ref, f32[2,1024]{1,0:T(2,128)} %b_out_ref.3, f32[2,1024]{1,0:T(2,128)} %b_down_ref.3, f32[1,512]{1,0:T(1,128)} %get-tuple-element.14.b_up_ref, ...), custom_call_target="tpu_custom_call" | custom-call | flops 22000001024 | bytes 10485760 | tf_op jit(solution)/shard_map/layer/pallas_call | solution.py:385
  139.4 125.5 %layer.3 = (f32[512,1024]{1,0:T(8,128)}, bf16[512,1024]{1,0:T(8,128)(2,1)}) custom-call(bf16[512,1024]{1,0:T(8,128)(2,1)} %get-tuple-element.8.h_ref, f32[512,1024]{1,0:T(8,128)} %get-tuple-element.9.res_ref, f32[8,1024]{1,0:T(8,128)} %reshape.6.norms_ref, f32[2,1024]{1,0:T(2,128)} %b_out_ref.3, f32[2,1024]{1,0:T(2,128)} %b_down_ref.3, ...), custom_call_target="tpu_custom_call" | custom-call | flops 22000001024 | bytes 10485760 | tf_op jit(solution)/shard_map/layer/pallas_call | solution.py:385
  264.9 2.3 copy.13
  (2 shorter events, 0.1 us)
Async XLA Ops:
  0.0 5.7 %copy-start = (bf16[2,1024,3,2,64]{1,4,3,2,0:T(8,128)(2,1)S(1)}, bf16[2,1024,3,2,64]{1,4,3,2,0:T(8,128)(2,1)}, u32[]{:S(2)}) copy-start(bf16[2,1024,3,2,64]{1,4,3,2,0:T(8,128)(2,1)} %param.11) | copy-start | bytes 4718596

commit v3 on v2

--- a/solution.py
+++ b/solution.py
@@ -12,7 +12,7 @@
 NT = (((1,), (1,)), ((), ()))
 VMEM_LIMIT = 63 * 2**20
 
-ME, SIB, LEFT, RIGHT, OPP, SLEFT, SRIGHT, SOPP = range(8)
+ME, SIB, LEFT, RIGHT, SLEFT, SRIGHT, OPP, SOPP = range(8)
 INVERSE = {SIB: SIB, LEFT: RIGHT, RIGHT: LEFT, OPP: OPP, SLEFT: SRIGHT, SRIGHT: SLEFT, SOPP: SOPP}
 ACROSS = {ME: SIB, LEFT: SLEFT, RIGHT: SRIGHT, OPP: SOPP}
 ORDER = [OPP, SOPP, LEFT, SLEFT, RIGHT, SRIGHT, SIB, ME]
@@ -22,7 +22,7 @@
 Z_CHUNKS = ['zu0', 'zu1', 'zd0', 'zd1']
 X_CHUNKS = Z_CHUNKS + ['cu', 'cd', 'co']
 TO_RIGHT = ['zu0', 'zd0', 'co', 'zu1', 'zd1', 'cu', 'cd']
-TO_LEFT = ['zu1', 'zd1', 'cu', 'zu0', 'zd0', 'cd', 'co']
+TO_LEFT = ['zu1', 'zd1', 'co', 'zu0', 'zd0', 'cu', 'cd']
 RELAY_RIGHT = ['zu0', 'zd0', 'co']
 RELAY_LEFT = ['zu1', 'zd1', 'cu', 'cd']
 
@@ -39,7 +39,7 @@
 
 
 def norm_kernel(rows_ref, norms_ref, out_ref):
-    out_ref[...] = layer_norm(rows_ref[...].astype(jnp.float32), norms_ref[0:1, :], norms_ref[1:2, :])
+    out_ref[...] = layer_norm(rows_ref[...].astype(jnp.float32), norms_ref[0, 0:1, :], norms_ref[0, 1:2, :])
 
 
 def norm_rows(rows, norms):
@@ -72,9 +72,9 @@
 KEYS = {key: i for i, key in enumerate(message_keys())}
 
 
-def layer_kernel(layer, last, group_size, qt, kc, h_ref, res_ref, norms_ref, b_out_ref, b_down_ref, b_up_ref, wqk_ref, wvt_ref,
+def layer_kernel(layer, last, group_size, qt, kc, h_ref, res_ref, norms_ref, b_out_ref, b_down_ref, b_up_ref, wqkv_ref,
                  w_out_ref, w_up_ref, w_down_ref, r_ref, hn_ref,
-                 x_v, wo_v, wu_v, wd_v, bu_v, q_s, k_s, vt_s, s_s, acc_s, o_loc, o_rcv, h2_s, send_sems, recv_sems, own_sems):
+                 x_v, wo_v, wu_v, wd_v, bu_v, q_s, k_s, vt_s, s_s, acc_s, o_loc, o_rcv, h2_s, wvt_s, send_sems, recv_sems, own_sems):
     rows, width = h_ref.shape
     ff = w_up_ref.shape[-1]
     seq = q_s.shape[0]
@@ -82,7 +82,6 @@
     n_heads = 2
     head_dim = pair // n_heads
     scale = head_dim ** -0.5 * LOG2E
-    base = 4 * layer
 
     me = lax.axis_index('tp')
     chip, core = me // 2, me % 2
@@ -185,15 +184,41 @@
     for rel in INVERSE:
         start('b', rel)
 
+    wvt_s[...] = wqkv_ref[:, 2 * pair:].T
     vt_s[:, head_dim:, :] = jnp.ones((n_heads, vt_s.shape[1] - head_dim, seq), jnp.bfloat16)
+
+    def own(i):
+        start('wr', TO_RIGHT[i])
+        start('wl', TO_LEFT[i])
+
+    def near(i):
+        for kind, relay, rel, c, relayed in (('wr', 'wrr', LEFT, TO_RIGHT[i], RELAY_RIGHT), ('wl', 'wll', RIGHT, TO_LEFT[i], RELAY_LEFT)):
+            recv(kind, c)
+            if c in relayed:
+                start(relay, c)
+            if c in Z_CHUNKS:
+                start('wz', rel, c)
+            start('wfx', rel, c)
+
+    def opposite(chunks):
+        for c in chunks:
+            recv('wrr' if c in RELAY_RIGHT else 'wll', c)
+            if c in Z_CHUNKS:
+                start('wz', OPP, c)
+            start('wfx', OPP, c)
+
+    def handed(rel, chunks):
+        for c in chunks:
+            recv('wz', rel, c)
+            start('wfz', rel, c)
 
     def project(rel):
         place = slice(PLACE[rel] * rows, (PLACE[rel] + 1) * rows)
         xr = h_ref[...] if rel == ME else x_v[rel]
-        qk = jnp.dot(xr, wqk_ref[...], preferred_element_type=jnp.float32)
+        qk = jnp.dot(xr, wqkv_ref[:, :2 * pair], preferred_element_type=jnp.float32)
         q_s[place, :] = qk[:, :pair].astype(jnp.bfloat16)
         k_s[place, :] = qk[:, pair:].astype(jnp.bfloat16)
-        vt = lax.dot_general(wvt_ref[...], xr, NT, preferred_element_type=jnp.float32).astype(jnp.bfloat16)
+        vt = lax.dot_general(wvt_s[...], xr, NT, preferred_element_type=jnp.float32).astype(jnp.bfloat16)
         for h in range(n_heads):
             vt_s[h, :head_dim, place] = vt[h * head_dim:(h + 1) * head_dim]
 
@@ -214,8 +239,7 @@
             for copy in own_copies():
                 copy.wait()
             for i in range(2):
-                start('wr', TO_RIGHT[i])
-                start('wl', TO_LEFT[i])
+                own(i)
             for a in ('u', 'd', 'o'):
                 start('ws', a)
     project(LEFT)
@@ -234,44 +258,17 @@
         recv('xs', OPP, p)
     project(SOPP)
 
-    def own(i):
-        start('wr', TO_RIGHT[i])
-        start('wl', TO_LEFT[i])
-
-    def near(i):
-        for kind, relay, rel, c, relayed in (('wr', 'wrr', LEFT, TO_RIGHT[i], RELAY_RIGHT), ('wl', 'wll', RIGHT, TO_LEFT[i], RELAY_LEFT)):
-            recv(kind, c)
-            if c in relayed:
-                start(relay, c)
-            if c in Z_CHUNKS:
-                start('wz', rel, c)
-            start('wfx', rel, c)
-
-    def opposite(chunks):
-        for c in chunks:
-            recv('wrr' if c in RELAY_RIGHT else 'wll', c)
-            if c in Z_CHUNKS:
-                start('wz', OPP, c)
-            start('wfx', OPP, c)
-
-    def handed(rel, chunks):
-        for c in chunks:
-            recv('wz', rel, c)
-            start('wfz', rel, c)
-
     ticks = {
-        1: [lambda: own(2)],
-        2: [lambda: near(0), lambda: own(3)],
-        4: [lambda: near(1), lambda: own(4)],
-        6: [lambda: near(2), lambda: own(5)],
-        7: [lambda: handed(LEFT, ['zu0']), lambda: handed(RIGHT, ['zu1'])],
-        8: [lambda: opposite(['zu0', 'zu1']), lambda: own(6)],
-        9: [lambda: near(3)],
-        10: [lambda: handed(LEFT, ['zd0']), lambda: handed(RIGHT, ['zd1'])],
-        11: [lambda: opposite(['zd0', 'zd1'])],
-        12: [lambda: near(4)],
-        14: [lambda: opposite(['cu', 'co'])],
-        15: [lambda: handed(OPP, ['zu0', 'zu1'])],
+        0: [lambda: near(0), lambda: own(2)],
+        2: [lambda: near(1), lambda: own(3)],
+        4: [lambda: near(2), lambda: own(4)],
+        5: [lambda: handed(LEFT, ['zu0']), lambda: handed(RIGHT, ['zu1'])],
+        6: [lambda: opposite(['zu0', 'zu1'])],
+        7: [lambda: own(5)],
+        8: [lambda: near(3), lambda: handed(LEFT, ['zd0']), lambda: handed(RIGHT, ['zd1'])],
+        10: [lambda: opposite(['zd0', 'zd1']), lambda: own(6)],
+        12: [lambda: near(4), lambda: opposite(['co'])],
+        14: [lambda: handed(OPP, ['zu0', 'zu1'])],
     }
     for i, rel in enumerate(ORDER[:-1]):
         ticks.setdefault(2 * i + 3, []).insert(0, lambda rel=rel: start('o', rel))
@@ -314,11 +311,6 @@
 
     lax.fori_loop(0, n_tiles, tile, 0)
 
-    near(5)
-    near(6)
-    opposite(['cd'])
-    handed(LEFT, ['zu1'])
-    handed(RIGHT, ['zu0'])
     recv('ws', 'o')
     for rel in (LEFT, RIGHT, OPP):
         recv('wfx', rel, 'co')
@@ -331,7 +323,10 @@
     attn_out = jnp.dot(heads, wo_v[...].reshape(width, width), preferred_element_type=jnp.float32)
     r = res_ref[...].astype(jnp.float32) + attn_out + b_out_ref[layer:layer + 1, :]
     r_ref[...] = r
-    h2_s[...] = layer_norm(r, norms_ref[base + 2:base + 3, :], norms_ref[base + 3:base + 4, :])
+    h2_s[...] = layer_norm(r, norms_ref[layer, 2:3, :], norms_ref[layer, 3:4, :])
+
+    near(5)
+    near(6)
 
     def arrive_across(rel):
         for c in X_CHUNKS:
@@ -342,13 +337,17 @@
 
     def before(rel):
         if rel == SIB:
+            handed(LEFT, ['zu1'])
+            handed(RIGHT, ['zu0'])
             recv('ws', 'u')
             recv('ws', 'd')
-            handed(OPP, ['zd0', 'zd1'])
+            opposite(['cu'])
         elif rel == LEFT:
+            opposite(['cd'])
             handed(LEFT, ['zd1'])
             handed(RIGHT, ['zd0'])
         elif rel == SLEFT:
+            handed(OPP, ['zd0', 'zd1'])
             arrive_across(LEFT)
         elif rel == SRIGHT:
             arrive_across(RIGHT)
@@ -370,12 +369,12 @@
         hn_ref[...] = r.astype(jnp.bfloat16)
     else:
         r_ref[...] = r
-        hn_ref[...] = layer_norm(r, norms_ref[base + 4:base + 5, :], norms_ref[base + 5:base + 6, :])
+        hn_ref[...] = layer_norm(r, norms_ref[layer + 1, 0:1, :], norms_ref[layer + 1, 1:2, :])
     for key in KEYS:
         message(key).wait_send()
 
 
-def run_layer(layer, last, group_size, head_dim, h, res, norms, b_out, b_down, b_up, wqk, wvt, w_out, w_up, w_down, qt=256, kc=512):
+def run_layer(layer, last, group_size, head_dim, h, res, norms, b_out, b_down, b_up, wqkv, w_out, w_up, w_down, qt=256, kc=512):
     rows, width = h.shape
     ff = w_up.shape[-1]
     seq = rows * group_size
@@ -385,7 +384,7 @@
     return pl.pallas_call(
         functools.partial(layer_kernel, layer, last, group_size, qt, kc),
         out_shape=(jax.ShapeDtypeStruct((rows, width), f32), jax.ShapeDtypeStruct((rows, width), bf16)),
-        in_specs=[whole()] * 8 + [anywhere] * 3,
+        in_specs=[whole()] * 7 + [anywhere] * 3,
         out_specs=(whole(), whole()),
         scratch_shapes=[
             pltpu.VMEM((group_size, rows, width), bf16),
@@ -401,6 +400,7 @@
             pltpu.VMEM((seq, pair), bf16),
             pltpu.VMEM((group_size, rows, pair), bf16),
             pltpu.VMEM((rows, width), bf16),
+            pltpu.VMEM((pair, width), bf16),
             pltpu.SemaphoreType.DMA((len(KEYS),)),
             pltpu.SemaphoreType.DMA((len(KEYS),)),
             pltpu.SemaphoreType.DMA((3,)),
@@ -408,7 +408,7 @@
         compiler_params=pltpu.CompilerParams(collective_id=layer, has_side_effects=True, vmem_limit_bytes=VMEM_LIMIT),
         cost_estimate=pl.CostEstimate(flops=22 * 10**9, bytes_accessed=10 * 2**20, transcendentals=2 * seq * seq),
         name='layer',
-    )(h, res, norms, b_out, b_down, b_up, wqk, wvt, w_out, w_up, w_down)
+    )(h, res, norms, b_out, b_down, b_up, wqkv, w_out, w_up, w_down)
 
 
 def solution(mesh):
@@ -417,15 +417,13 @@
     def local_layers(hidden_in, norms, w_qkv, w_out, b_out, w_up, b_up, w_down, b_down):
         n_layers, width, slots, heads_loc, head_dim = w_qkv.shape
         pair = heads_loc * head_dim
-        norms = norms.reshape(n_layers * 4, width)
         w_out = w_out.reshape(n_layers, pair, width)
         residual = hidden_in[0]
         normed = norm_rows(residual, norms)
         for layer in range(n_layers):
-            w_l = w_qkv[layer].reshape(width, slots * pair)
-            wqk, wvt = w_l[:, :2 * pair], w_l[:, 2 * pair:].T
+            wqkv = w_qkv[layer].reshape(width, slots * pair)
             residual, normed = run_layer(layer, layer == n_layers - 1, group_size, head_dim, normed, residual, norms, b_out, b_down,
-                                         b_up[layer:layer + 1], wqk, wvt, w_out, w_up, w_down)
+                                         b_up[layer:layer + 1], wqkv, w_out, w_up, w_down)
         return normed[None]
 
     in_specs = (P('dp', 'tp', None), P(), P(None, None, None, 'tp', None), P(None, 'tp', None, None), P(), P(None, None, 'tp'), P(None, 'tp'), P(None, 'tp', None), P())

time: 267 us -> 262 us (0.981)
    pallas_call x2, Pallas kernels: 255 us -> 253 us  [run_layer(): pl.pallas_call(functools.partial(layer_kernel, layer, last, group_size, q...]
where the time goes in v3:
time: 262 us
  Pallas kernels  256 us (98%)
  local copies, waits for them, and re-layouts  6.15 us (2%)
    pallas_call x2, Pallas kernels, run_layer(): pl.pallas_call(functools.partial(layer_kernel, layer, last, group_size, q...  253 us

profile of v3, /device:TPU:81, one launch (start us, length us, event | category | flops | bytes accessed | tf_op | source)
XLA Modules:
  0.0 261.8 jit_solution(18329356201083226631)
XLA Ops:
  0.0 0.0 copy-start
  0.0 1.4 fusion.1
  1.4 2.9 %norm_rows.1.h_ref = bf16[512,1024]{1,0:T(8,128)(2,1)} custom-call(bf16[512,1024]{1,0:T(8,128)(2,1)} %bitcast.7, f32[2,4,1024]{2,1,0:T(4,128)} %norms_ref.5), custom_call_target="tpu_custom_call" | custom-call | flops 5242880 | bytes 2097152 | tf_op jit(solution)/shard_map/norm_rows/pallas_call | solution.py:46
  4.4 0.0 copy-done
  4.4 0.1 fusion
  4.5 1.1 copy.13.wqkv_ref
  5.6 1.2 copy.12.wqkv_ref
  6.8 126.5 %layer.2 = (f32[512,1024]{1,0:T(8,128)}, bf16[512,1024]{1,0:T(8,128)(2,1)}) custom-call(bf16[512,1024]{1,0:T(8,128)(2,1)} %norm_rows.1.h_ref, bf16[512,1024]{1,0:T(8,128)(2,1)} %bitcast.8, f32[2,4,1024]{2,1,0:T(4,128)} %norms_ref.5, f32[2,1024]{1,0:T(2,128)} %b_out_ref.3, f32[2,1024]{1,0:T(2,128)} %b_down_ref.3, f32[1,512]{1,0:T(1,128)} %get-tuple-element.14.b_up_ref, ...), custom_call_target="tpu_custom_call" | custom-call | flops 22000001024 | bytes 10485760 | tf_op jit(solution)/shard_map/layer/pallas_call | solution.py:384
  133.3 126.2 %layer.3 = (f32[512,1024]{1,0:T(8,128)}, bf16[512,1024]{1,0:T(8,128)(2,1)}) custom-call(bf16[512,1024]{1,0:T(8,128)(2,1)} %get-tuple-element.8.h_ref, f32[512,1024]{1,0:T(8,128)} %get-tuple-element.9.res_ref, f32[2,4,1024]{2,1,0:T(4,128)} %norms_ref.5, f32[2,1024]{1,0:T(2,128)} %b_out_ref.3, f32[2,1024]{1,0:T(2,128)} %b_down_ref.3, ...), custom_call_target="tpu_custom_call" | custom-call | flops 22000001024 | bytes 10485760 | tf_op jit(solution)/shard_map/layer/pallas_call | solution.py:384
  259.5 2.3 copy.15
Async XLA Ops:
  0.0 4.4 %copy-start = (bf16[2,1024,3,2,64]{1,4,3,2,0:T(8,128)(2,1)S(1)}, bf16[2,1024,3,2,64]{1,4,3,2,0:T(8,128)(2,1)}, u32[]{:S(2)}) copy-start(bf16[2,1024,3,2,64]{1,4,3,2,0:T(8,128)(2,1)} %param.11) | copy-start | bytes 4718596
